TPU v7x, 32 devices: a whole 2x2x4 slice. The times are simulated.
32 devices in a mesh: zero: 8 (over z, x), tp: 4 (over y, core).
Axes of the slice: x: 2, y: 2, z: 4, core: 2. Of those that a mesh axis runs over, the one named last changes fastest.
Arguments:
- train_gate: float32 [2048, 8192], P('zero', 'tp'), may hold values from -0.1875 to 0.1875
- slow_gate: float32 [2048, 8192], P('zero', 'tp'), may hold values from -0.125 to 0.125
- train_up: float32 [2048, 8192], P('zero', 'tp'), may hold values from -0.1875 to 0.1875
- slow_up: float32 [2048, 8192], P('zero', 'tp'), may hold values from -0.125 to 0.125
- norm_gain: float32 [2048], P('zero'), may hold values from 0.25 to 1.75
Outputs:
- serving_gate: bfloat16 [2048, 8192], P(None, 'tp')
- serving_up: bfloat16 [2048, 8192], P(None, 'tp')
- scale_gate: float32 [8192], P('tp')
- scale_up: float32 [8192], P('tp')
All inputs are finite; a program needn't handle non-finite values.
Results may differ from a plain program's by a relative error of at most 0.0004.
Values may be sent and summed in bfloat16 or wider, within the bound.
A program may use at most 128 MiB of HBM per device.

v0:
```python
import jax
import jax.numpy as jnp
from jax import lax
from jax.sharding import PartitionSpec as P

keep_rate = 0.75


def body(train_gate, slow_gate, train_up, slow_up, norm_gain):
    whole_gate = keep_rate * slow_gate + (1.0 - keep_rate) * train_gate
    whole_up = keep_rate * slow_up + (1.0 - keep_rate) * train_up
    whole_gained_gate = whole_gate * norm_gain[:, None]
    whole_gained_up = whole_up * norm_gain[:, None]
    total_gate, total_up = lax.psum(
        (
            jnp.sum(whole_gained_gate * whole_gained_gate, axis=0),
            jnp.sum(whole_gained_up * whole_gained_up, axis=0),
        ),
        "zero",
    )
    scale_gate = jnp.sqrt(total_gate)
    scale_up = jnp.sqrt(total_up)
    narrow_gate, narrow_up = (
        (whole_gained_gate / scale_gate).astype(jnp.bfloat16),
        (whole_gained_up / scale_up).astype(jnp.bfloat16),
    )
    serving_gate, serving_up = (
        lax.all_gather(narrow_gate, "zero", axis=0, tiled=True),
        lax.all_gather(narrow_up, "zero", axis=0, tiled=True),
    )
    return (serving_gate, serving_up, scale_gate, scale_up)


def solution(mesh):
    in_specs = (P("zero", "tp"), P("zero", "tp"), P("zero", "tp"), P("zero", "tp"), P("zero"))
    out_specs = (P(None, "tp"), P(None, "tp"), P("tp"), P("tp"))
    return jax.shard_map(body, mesh=mesh, in_specs=in_specs, out_specs=out_specs, check_vma=False)
```

profile of v0, /device:TPU:0, one launch (start us, length us, event | category | flops | bytes accessed | tf_op | source)
XLA Modules:
  0.0 327.2 jit_solution(7934663206639320747)
XLA Ops:
  7.2 0.0 copy-start.3
  7.2 0.0 copy-start
  7.2 0.0 all-gather.5.cloned.1.call-start
  7.2 4.7 %multiply_reduce_fusion = (f32[2048]{0:T(1024)S(1)}, f32[2048]{0:T(1024)S(1)}) fusion(f32[256]{0:T(256)} %param.9, f32[256,2048]{1,0:T(8,128)} %param.7, f32[256,2048]{1,0:T(8,128)} %param.8, f32[256,2048]{1,0:T(8,128)} %param.5, f32[256,2048]{1,0:T(8,128)} %param.6), kind=kLoop, calls=%fused_computation.1 | loop fusion | flops 6287360 | bytes 8406016 | tf_op jit(solution)/shard_map/reduce_sum | solution.py:17
  12.0 38.8 %all-reduce = (f32[2048]{0:T(1024)S(1)}, f32[2048]{0:T(1024)S(1)}) all-reduce(f32[2048]{0:T(1024)S(1)} %get-tuple-element.5, f32[2048]{0:T(1024)S(1)} %get-tuple-element.4), channel_id=1, replica_groups=mesh['zero'=8,'tp'=4] {'zero'}, use_global_device_ids=true, to_apply=%region_1.0 | all-reduce | flops 4096 | bytes 32768 | tf_op jit(solution)/shard_map/psum | solution.py:14
  50.8 0.0 copy-start.1
  50.8 0.0 copy-done.3
  50.9 0.0 copy-done
  50.9 0.0 copy-start.2
  50.9 5.3 %divide_convert_fusion = (bf16[256,2048]{1,0:T(8,128)(2,1)}, bf16[256,2048]{1,0:T(8,128)(2,1)}) fusion(f32[2048]{0:T(1024)S(1)} %sqrt.7, f32[256]{0:T(256)S(1)} %copy-done.3, f32[256,2048]{1,0:T(8,128)S(1)} %copy-done, f32[256,2048]{1,0:T(8,128)} %param.8, f32[2048]{0:T(1024)S(1)} %sqrt.6, f32[256,2048]{1,0:T(8,128)} %param.5, f32[256,2048]{1,0:T(8,128)} %param.6), kind=kLoop, calls=%fused_computation | loop fusion | flops 6291456 | bytes 10503168 | tf_op jit(solution)/shard_map/convert_element_type | solution.py:25
  56.2 0.0 copy-done.1
  56.2 0.0 copy-done.2
  56.2 0.0 all-gather.5.cloned.1.call-update
  56.2 0.0 all-gather.3.cloned.1.call-start
  56.3 0.7 all-gather.3.cloned.1.call-update
  57.0 121.2 %all-gather.5.cloned.1.call-done = bf16[2048,2048]{1,0:T(8,128)(2,1)} async-done(((bf16[256,2048]{1,0:T(8,128)(2,1)}), bf16[2048,2048]{1,0:T(8,128)(2,1)}) %all-gather.5.cloned.1.call-update) | async-done | bytes 8388624 | tf_op jit(solution)/shard_map/all_gather | solution.py:29
  178.1 125.4 %all-gather.3.cloned.1.call-done = bf16[2048,2048]{1,0:T(8,128)(2,1)} async-done(((bf16[256,2048]{1,0:T(8,128)(2,1)}), bf16[2048,2048]{1,0:T(8,128)(2,1)}) %all-gather.3.cloned.1.call-update) | async-done | bytes 8388624 | tf_op jit(solution)/shard_map/all_gather | solution.py:28
  303.5 8.4 %copy.11 = bf16[2048,2048]{1,0:T(8,128)(2,1)} copy(bf16[2048,2048]{1,0:T(8,128)(2,1)} %all-gather.3.cloned.1.call-done) | data formatting | bytes 16777216
  312.0 8.4 %copy.12 = bf16[2048,2048]{1,0:T(8,128)(2,1)} copy(bf16[2048,2048]{1,0:T(8,128)(2,1)} %all-gather.5.cloned.1.call-done) | data formatting | bytes 16777216
  (2 shorter events, 0.0 us)
Async XLA Ops:
  7.2 43.7 %copy-start.3 = (f32[256]{0:T(256)S(1)}, f32[256]{0:T(256)}, u32[]{:S(2)}) copy-start(f32[256]{0:T(256)} %param.9) | copy-start | bytes 3076
  7.2 43.7 %copy-start = (f32[256,2048]{1,0:T(8,128)S(1)}, f32[256,2048]{1,0:T(8,128)}, u32[]{:S(2)}) copy-start(f32[256,2048]{1,0:T(8,128)} %param.7) | copy-start | bytes 6291460
  7.2 170.9 %all-gather.5.cloned.1.call-start = ((), (), s32[]{:S(2)}) async-start(), calls=%async_computation.1 | async-start | bytes 9437184 | tf_op jit(solution)/shard_map/all_gather | solution.py:29
  50.8 5.4 %copy-start.1 = (f32[2048]{0:T(1024)}, f32[2048]{0:T(1024)S(1)}, u32[]{:S(2)}) copy-start(f32[2048]{0:T(1024)S(1)} %sqrt.6) | copy-start | bytes 24580
  50.9 5.3 %copy-start.2 = (f32[2048]{0:T(1024)}, f32[2048]{0:T(1024)S(1)}, u32[]{:S(2)}) copy-start(f32[2048]{0:T(1024)S(1)} %sqrt.7) | copy-start | bytes 24580
  56.2 247.3 %all-gather.3.cloned.1.call-start = ((), (), s32[]{:S(2)}) async-start(), calls=%async_computation | async-start | bytes 9437184 | tf_op jit(solution)/shard_map/all_gather | solution.py:28
Sparse Core Ops, SparseCore 0:
  56.3 121.7 all-gather.4
  180.8 122.6 all-gather.2
where the time goes:
time: 327 us
  waiting for transfers between devices  247 us (76%)
  blocking collectives  38.8 us (12%)
  local copies, waits for them, and re-layouts  16.9 us (5%)
  between operations  14.1 us (4%)
  other arithmetic  10 us (3%)
    all_gather x1, waiting for transfers between devices, body(): lax.all_gather(narrow_gate, 'zero', axis=0, tiled=True)  125 us
    all_gather x1, waiting for transfers between devices, body(): lax.all_gather(narrow_up, 'zero', axis=0, tiled=True)  121 us
    psum x1, blocking collectives, body(): lax.psum((jnp.sum(whole_gained_gate * whole_gained_gate, axis=0), jnp.sum...  38.8 us
    unnamed x10, local copies, waits for them, and re-layouts  16.9 us
  transfers between devices with their start and end apart: 2, of which 2 were waited for; matrix products, arithmetic and copies ran while one was open for 0% of the time, Pallas kernels for 0%

commit v1 on v0

v1 whole, which is shorter than its diff:
```python
import functools

import jax
import jax.numpy as jnp
from jax import lax
from jax.experimental import pallas as pl
from jax.experimental.pallas import tpu as pltpu
from jax.sharding import PartitionSpec as P

keep_rate = 0.75
MESH = pl.DeviceIdType.MESH
SIDE = 2


def gather_kernel(
    count, pieces,
    train_gate, slow_gate, train_up, slow_up, gain_ref,
    gate_ref, up_ref, scale_gate_ref, scale_up_ref,
    train, slow, sums,
    load_sem, sum_send, sum_recv,
    left_send, left_recv, right_send, right_recv, side_send, side_recv, half_send, half_recv,
):
    length = count // SIDE
    rows = train_gate.shape[0]
    piece_rows = rows // pieces
    me = lax.axis_index("zero")
    place, side = me // SIDE, me % SIDE
    outs = (gate_ref, up_ref)

    loads = []
    for which, (t, s) in enumerate(((train_gate, slow_gate), (train_up, slow_up))):
        for p in range(pieces):
            at = pl.ds(p * piece_rows, piece_rows)
            k = (which * pieces + p) * 2
            loads.append((
                pltpu.make_async_copy(t.at[at], train.at[which, at], load_sem.at[k]),
                pltpu.make_async_copy(s.at[at], slow.at[which, at], load_sem.at[k + 1]),
            ))
    for pair in loads:
        for load in pair:
            load.start()

    barrier = pltpu.get_barrier_semaphore()
    for step in range(1, count):
        pl.semaphore_signal(barrier, 1, device_id={"zero": lax.rem(me + step, count)}, device_id_type=MESH)

    for which in range(2):
        total = None
        for p in range(pieces):
            for load in loads[which * pieces + p]:
                load.wait()
            at = pl.ds(p * piece_rows, piece_rows)
            gained = (keep_rate * slow[which, at, :] + (1.0 - keep_rate) * train[which, at, :]) * gain_ref[at, :]
            slow[which, at, :] = gained
            part = jnp.sum(gained * gained, axis=0, keepdims=True)
            total = part if total is None else total + part
        sums[me, pl.ds(which, 1), :] = total

    pl.semaphore_wait(barrier, count - 1)
    sum_copies = []
    for step in range(1, count):
        copy = pltpu.make_async_remote_copy(
            src_ref=sums.at[me], dst_ref=sums.at[me],
            send_sem=sum_send.at[step - 1], recv_sem=sum_recv.at[step - 1],
            device_id={"zero": lax.rem(me + step, count)}, device_id_type=MESH,
        )
        copy.start()
        sum_copies.append(copy)
    for step in range(1, count):
        source = lax.rem(me + count - step, count)
        pltpu.make_async_remote_copy(
            src_ref=sums.at[source], dst_ref=sums.at[source],
            send_sem=sum_send.at[step - 1], recv_sem=sum_recv.at[step - 1],
            device_id={"zero": source}, device_id_type=MESH,
        ).wait_recv()
    total = sums[0]
    for k in range(1, count):
        total = total + sums[k]
    scale = jnp.sqrt(total)
    scale_gate_ref[...] = scale[0:1]
    scale_up_ref[...] = scale[1:2]
    inverse = 1.0 / scale

    def part_of(owner_place, owner_side, which, p):
        start = (owner_place * SIDE + owner_side) * rows + p * piece_rows
        return outs[which].at[pl.ds(pl.multiple_of(start, piece_rows), piece_rows)]

    def copy_to(ref, send, recv, to):
        return pltpu.make_async_remote_copy(
            src_ref=ref, dst_ref=ref, send_sem=send, recv_sem=recv,
            device_id={"zero": to}, device_id_type=MESH,
        )

    to_left = jnp.maximum(place - 1, 0) * SIDE + side
    to_right = jnp.minimum(place + 1, length - 1) * SIDE + side
    to_side = place * SIDE + (SIDE - 1 - side)
    has_left, has_right = place > 0, place < length - 1
    is_even = place % 2 == 0
    twin = place + 1 - 2 * (place % 2)
    to_twin = twin * SIDE + side
    order = [(which, p) for which in range(2) for p in range(pieces)]

    def left_copy(distance, which, p):
        k = distance * 2 * pieces + which * pieces + p
        return copy_to(part_of(place + distance, side, which, p), left_send.at[k], left_recv.at[k], to_left)

    def right_copy(distance, which, p):
        k = distance * 2 * pieces + which * pieces + p
        return copy_to(part_of(place - distance, side, which, p), right_send.at[k], right_recv.at[k], to_right)

    def side_index(distance, which, p):
        d = distance if distance >= 0 else length - 1 - distance
        return d * 2 * pieces + which * pieces + p

    def side_copy(distance, which, p):
        k = side_index(distance, which, p)
        return copy_to(part_of(place + distance, side, which, p), side_send.at[k], side_recv.at[k], to_side)

    def side_arrival(distance, which, p):
        k = side_index(distance, which, p)
        return copy_to(part_of(place + distance, SIDE - 1 - side, which, p), side_send.at[k], side_recv.at[k], to_side)

    def half_copy(p):
        return copy_to(part_of(place, SIDE - 1 - side, 1, p), half_send.at[p], half_recv.at[p], to_twin)

    def half_arrival(p):
        return copy_to(part_of(twin, SIDE - 1 - side, 1, p), half_send.at[p], half_recv.at[p], to_twin)

    def in_line(distance):
        return place + distance <= length - 1 if distance > 0 else place + distance >= 0

    def by_side(distance, which):
        ok = in_line(distance)
        if which == 1 and distance == 1:
            ok = jnp.logical_and(ok, jnp.logical_not(is_even))
        if which == 1 and distance == -1:
            ok = jnp.logical_and(ok, is_even)
        return ok

    def send_own(which, p):
        @pl.when(has_left)
        def _():
            left_copy(0, which, p).start()

        @pl.when(has_right)
        def _():
            right_copy(0, which, p).start()

        side_copy(0, which, p).start()

    previous = None
    for which, p in order:
        at = pl.ds(p * piece_rows, piece_rows)
        start = pl.multiple_of(me * rows + p * piece_rows, piece_rows)
        outs[which][pl.ds(start, piece_rows), :] = (slow[which, at, :] * inverse[which:which + 1]).astype(jnp.bfloat16)
        if previous is not None:
            send_own(*previous)
        previous = (which, p)
    send_own(*previous)

    for k in range(1, length):
        for which, p in order:
            @pl.when(in_line(k))
            def _():
                q = (k - 1) * 2 * pieces + which * pieces + p
                copy_to(part_of(place + k, side, which, p), left_send.at[q], left_recv.at[q], to_right).wait_recv()

                @pl.when(has_left)
                def _():
                    left_copy(k, which, p).start()

            @pl.when(by_side(k, which))
            def _():
                side_copy(k, which, p).start()

            @pl.when(in_line(-k))
            def _():
                q = (k - 1) * 2 * pieces + which * pieces + p
                copy_to(part_of(place - k, side, which, p), right_send.at[q], right_recv.at[q], to_left).wait_recv()

                @pl.when(has_right)
                def _():
                    right_copy(k, which, p).start()

            @pl.when(by_side(-k, which))
            def _():
                side_copy(-k, which, p).start()

    for which, p in order:
        side_arrival(0, which, p).wait_recv()
        if which == 1:
            half_copy(p).start()

    for k in range(1, length):
        for which, p in order:
            for distance in (k, -k):
                @pl.when(by_side(distance, which))
                def _():
                    side_arrival(distance, which, p).wait_recv()
                    side_copy(distance, which, p).wait_send()

    for p in range(pieces):
        half_arrival(p).wait_recv()
        half_copy(p).wait_send()

    for copy in sum_copies:
        copy.wait_send()
    for which, p in order:
        side_copy(0, which, p).wait_send()
        for k in range(length):
            @pl.when(jnp.logical_and(has_left, place + k <= length - 1))
            def _():
                left_copy(k, which, p).wait_send()

            @pl.when(jnp.logical_and(has_right, place - k >= 0))
            def _():
                right_copy(k, which, p).wait_send()


def solution(mesh):
    count = mesh.shape["zero"]

    def body(train_gate, slow_gate, train_up, slow_up, norm_gain):
        rows, columns = train_gate.shape
        pieces = max(1, min(4, rows // 64))
        length = count // SIDE
        block = pltpu.VMEM((rows * count, columns), jnp.bfloat16)
        scale = jax.ShapeDtypeStruct((1, columns), jnp.float32)
        vmem, held = pl.BlockSpec(memory_space=pltpu.VMEM), pl.BlockSpec(memory_space=pltpu.HBM)
        dma = lambda n: pltpu.SemaphoreType.DMA((n,))
        line, wide = length * 2 * pieces, (2 * length - 1) * 2 * pieces
        gate, up, scale_gate, scale_up = pl.pallas_call(
            functools.partial(gather_kernel, count, pieces),
            out_shape=(block, block, scale, scale),
            in_specs=[held] * 4 + [vmem],
            out_specs=(vmem,) * 4,
            scratch_shapes=[
                pltpu.VMEM((2, rows, columns), jnp.float32),
                pltpu.VMEM((2, rows, columns), jnp.float32),
                pltpu.VMEM((count, 2, columns), jnp.float32),
                dma(4 * pieces), dma(count - 1), dma(count - 1),
                dma(line), dma(line), dma(line), dma(line), dma(wide), dma(wide), dma(pieces), dma(pieces),
            ],
            compiler_params=pltpu.CompilerParams(
                collective_id=0, has_side_effects=True, vmem_limit_bytes=24 << 20
            ),
        )(train_gate, slow_gate, train_up, slow_up, norm_gain[:, None])
        return gate, up, scale_gate[0], scale_up[0]

    in_specs = (P("zero", "tp"), P("zero", "tp"), P("zero", "tp"), P("zero", "tp"), P("zero"))
    out_specs = (P(None, "tp"), P(None, "tp"), P("tp"), P("tp"))
    return jax.shard_map(body, mesh=mesh, in_specs=in_specs, out_specs=out_specs, check_vma=False)
```

time: 327 us -> 187 us (0.57)
  waiting for transfers between devices: 247 us -> 0 us
  Pallas kernels: 0 us -> 171 us
  blocking collectives: 38.8 us -> 0 us
  between operations: 14.1 us -> 0.66 us
  other arithmetic: 10 us -> 0 us
    all_gather x2 -> x0, waiting for transfers between devices: 247 us -> none  [the longest x1 125 us: body(): lax.all_gather(narrow_gate, 'zero', axis=0, tiled=True)]
    pallas_call x0 -> x1, Pallas kernels: none -> 171 us  [body(): pl.pallas_call(functools.partial(gather_kernel, count, pieces), out_shape...]
    psum x1 -> x0, blocking collectives: 38.8 us -> none  [body(): lax.psum((jnp.sum(whole_gained_gate * whole_gained_gate, axis=0), jnp.sum...]
    convert_element_type x1 -> x0, other arithmetic: 5.31 us -> none  [body(): (whole_gained_up / scale_up).astype(jnp.bfloat16)]
    reduce_sum x1 -> x0, other arithmetic: 4.73 us -> none  [body(): jnp.sum(whole_gained_up * whole_gained_up, axis=0)]
    unnamed x10 -> x12, local copies, waits for them, and re-layouts: 16.9 us -> 14.4 us
  transfers between devices with their start and end apart: 2 -> 0, of which waited for: 2 -> 0; matrix products, arithmetic and copies ran while one was open for 0% -> 0% of each run, Pallas kernels for 0% -> 0%
where the time goes in v1:
time: 187 us
  Pallas kernels  171 us (91%)
  local copies, waits for them, and re-layouts  15.2 us (8%)
    pallas_call x1, Pallas kernels, body(): pl.pallas_call(functools.partial(gather_kernel, count, pieces), out_shape...  171 us
    unnamed x12, local copies, waits for them, and re-layouts  14.4 us

profile of v1, /device:TPU:0, one launch (start us, length us, event | category | flops | bytes accessed | tf_op | source)
XLA Modules:
  0.0 186.8 jit_solution(5293267516868714996)
XLA Ops:
  0.6 0.8 copy.9.gain_ref
  1.4 0.0 copy-start
  1.5 1.6 copy-done
  3.0 0.0 copy-start.1
  3.0 1.6 copy-done.1
  4.6 0.0 copy-start.2
  4.6 1.6 copy-done.2
  6.2 0.0 copy-start.3
  6.2 1.6 copy-done.3
  7.8 171.0 %shard_map.84 = (bf16[2048,2048]{1,0:T(8,128)(2,1)S(1)}, bf16[2048,2048]{1,0:T(8,128)(2,1)S(1)}, f32[1,2048]{1,0:T(1,128)S(1)}, f32[1,2048]{1,0:T(1,128)S(1)}) custom-call(f32[256,2048]{1,0:T(8,128)S(1)} %copy-done, f32[256,2048]{1,0:T(8,128)S(1)} %copy-done.1, f32[256,2048]{1,0:T(8,128)S(1)} %copy-done.2, f32[256,2048]{1,0:T(8,128)S(1)} %copy-done.3, ...), custom_call_target="tpu_custom_call" | custom-call | tf_op jit(solution)/shard_map/pallas_call | solution.py:232
  178.9 3.4 %copy.14 = bf16[2048,2048]{1,0:T(8,128)(2,1)} copy(bf16[2048,2048]{1,0:T(8,128)(2,1)S(1)} %get-tuple-element.12) | data formatting | bytes 16777216
  182.3 3.4 %copy.15 = bf16[2048,2048]{1,0:T(8,128)(2,1)} copy(bf16[2048,2048]{1,0:T(8,128)(2,1)S(1)} %get-tuple-element.13) | data formatting | bytes 16777216
  185.6 0.6 copy.16
  186.2 0.6 copy.17
Async XLA Ops:
  1.4 1.6 copy-start
  3.0 1.6 copy-start.1
  4.6 1.6 copy-start.2
  6.2 1.6 copy-start.3

commit v2 on v1

--- a/solution.py
+++ b/solution.py
@@ -10,22 +10,26 @@
 keep_rate = 0.75
 MESH = pl.DeviceIdType.MESH
 SIDE = 2
+LANES = 128
+GROUP = 8
+VMEM_BYTES = 67_043_328
 
 
 def gather_kernel(
     count, pieces,
     train_gate, slow_gate, train_up, slow_up, gain_ref,
     gate_ref, up_ref, scale_gate_ref, scale_up_ref,
-    train, slow, sums,
+    train, slow, gains, sums,
     load_sem, sum_send, sum_recv,
     left_send, left_recv, right_send, right_recv, side_send, side_recv, half_send, half_recv,
 ):
     length = count // SIDE
-    rows = train_gate.shape[0]
+    rows, columns = train_gate.shape
     piece_rows = rows // pieces
     me = lax.axis_index("zero")
     place, side = me // SIDE, me % SIDE
     outs = (gate_ref, up_ref)
+    scales = (scale_gate_ref, scale_up_ref)
 
     loads = []
     for which, (t, s) in enumerate(((train_gate, slow_gate), (train_up, slow_up))):
@@ -44,42 +48,34 @@
     for step in range(1, count):
         pl.semaphore_signal(barrier, 1, device_id={"zero": lax.rem(me + step, count)}, device_id_type=MESH)
 
+    gains[...] = jnp.broadcast_to(gain_ref[...], (LANES, rows)).T
+
+    def sum_copy(which, step, source, to):
+        k = which * (count - 1) + step - 1
+        return pltpu.make_async_remote_copy(
+            src_ref=sums.at[which, source], dst_ref=sums.at[which, source],
+            send_sem=sum_send.at[k], recv_sem=sum_recv.at[k],
+            device_id={"zero": to}, device_id_type=MESH,
+        )
+
     for which in range(2):
-        total = None
+        def add(i, total):
+            at = pl.ds(pl.multiple_of(i * GROUP, GROUP), GROUP)
+            gain = jnp.concatenate([gains[at, :]] * (columns // LANES), axis=1)
+            gained = (keep_rate * slow[which, at, :] + (1.0 - keep_rate) * train[which, at, :]) * gain
+            slow[which, at, :] = gained
+            return total + gained * gained
+
+        total = jnp.zeros((GROUP, columns), jnp.float32)
         for p in range(pieces):
             for load in loads[which * pieces + p]:
                 load.wait()
-            at = pl.ds(p * piece_rows, piece_rows)
-            gained = (keep_rate * slow[which, at, :] + (1.0 - keep_rate) * train[which, at, :]) * gain_ref[at, :]
-            slow[which, at, :] = gained
-            part = jnp.sum(gained * gained, axis=0, keepdims=True)
-            total = part if total is None else total + part
-        sums[me, pl.ds(which, 1), :] = total
-
-    pl.semaphore_wait(barrier, count - 1)
-    sum_copies = []
-    for step in range(1, count):
-        copy = pltpu.make_async_remote_copy(
-            src_ref=sums.at[me], dst_ref=sums.at[me],
-            send_sem=sum_send.at[step - 1], recv_sem=sum_recv.at[step - 1],
-            device_id={"zero": lax.rem(me + step, count)}, device_id_type=MESH,
-        )
-        copy.start()
-        sum_copies.append(copy)
-    for step in range(1, count):
-        source = lax.rem(me + count - step, count)
-        pltpu.make_async_remote_copy(
-            src_ref=sums.at[source], dst_ref=sums.at[source],
-            send_sem=sum_send.at[step - 1], recv_sem=sum_recv.at[step - 1],
-            device_id={"zero": source}, device_id_type=MESH,
-        ).wait_recv()
-    total = sums[0]
-    for k in range(1, count):
-        total = total + sums[k]
-    scale = jnp.sqrt(total)
-    scale_gate_ref[...] = scale[0:1]
-    scale_up_ref[...] = scale[1:2]
-    inverse = 1.0 / scale
+            total = lax.fori_loop(p * piece_rows // GROUP, (p + 1) * piece_rows // GROUP, add, total)
+        sums[which, me] = jnp.sum(total, axis=0, keepdims=True)
+        if which == 0:
+            pl.semaphore_wait(barrier, count - 1)
+        for step in range(1, count):
+            sum_copy(which, step, me, lax.rem(me + step, count)).start()
 
     def part_of(owner_place, owner_side, which, p):
         start = (owner_place * SIDE + owner_side) * rows + p * piece_rows
@@ -148,15 +144,23 @@
 
         side_copy(0, which, p).start()
 
-    previous = None
-    for which, p in order:
-        at = pl.ds(p * piece_rows, piece_rows)
-        start = pl.multiple_of(me * rows + p * piece_rows, piece_rows)
-        outs[which][pl.ds(start, piece_rows), :] = (slow[which, at, :] * inverse[which:which + 1]).astype(jnp.bfloat16)
-        if previous is not None:
-            send_own(*previous)
-        previous = (which, p)
-    send_own(*previous)
+    for which in range(2):
+        for step in range(1, count):
+            source = lax.rem(me + count - step, count)
+            sum_copy(which, step, source, source).wait_recv()
+        total = sums[which, 0]
+        for k in range(1, count):
+            total = total + sums[which, k]
+        scale = jnp.sqrt(total)
+        scales[which][...] = scale
+        inverse = 1.0 / scale
+        for p in range(pieces + 1):
+            if p < pieces:
+                at = pl.ds(p * piece_rows, piece_rows)
+                start = pl.multiple_of(me * rows + p * piece_rows, piece_rows)
+                outs[which][pl.ds(start, piece_rows), :] = (slow[which, at, :] * inverse).astype(jnp.bfloat16)
+            if p > 0:
+                send_own(which, p - 1)
 
     for k in range(1, length):
         for which, p in order:
@@ -203,8 +207,9 @@
         half_arrival(p).wait_recv()
         half_copy(p).wait_send()
 
-    for copy in sum_copies:
-        copy.wait_send()
+    for which in range(2):
+        for step in range(1, count):
+            sum_copy(which, step, me, lax.rem(me + step, count)).wait_send()
     for which, p in order:
         side_copy(0, which, p).wait_send()
         for k in range(length):
@@ -217,6 +222,21 @@
                 right_copy(k, which, p).wait_send()
 
 
+def store_kernel(parts, gate, up, scale_gate, scale_up, gate_out, up_out, scale_gate_out, scale_up_out, sem):
+    rows = gate.shape[0] // parts
+    copies = []
+    for which, (held, out) in enumerate(((gate, gate_out), (up, up_out))):
+        for k in range(parts):
+            at = pl.ds(k * rows, rows)
+            copies.append(pltpu.make_async_copy(held.at[at], out.at[at], sem.at[which * parts + k]))
+    for copy in copies:
+        copy.start()
+    scale_gate_out[...] = scale_gate[0, :]
+    scale_up_out[...] = scale_up[0, :]
+    for copy in copies:
+        copy.wait()
+
+
 def solution(mesh):
     count = mesh.shape["zero"]
 
@@ -224,12 +244,13 @@
         rows, columns = train_gate.shape
         pieces = max(1, min(4, rows // 64))
         length = count // SIDE
-        block = pltpu.VMEM((rows * count, columns), jnp.bfloat16)
-        scale = jax.ShapeDtypeStruct((1, columns), jnp.float32)
+        full = (rows * count, columns)
+        block = pltpu.VMEM(full, jnp.bfloat16)
+        scale = pltpu.VMEM((1, columns), jnp.float32)
         vmem, held = pl.BlockSpec(memory_space=pltpu.VMEM), pl.BlockSpec(memory_space=pltpu.HBM)
         dma = lambda n: pltpu.SemaphoreType.DMA((n,))
         line, wide = length * 2 * pieces, (2 * length - 1) * 2 * pieces
-        gate, up, scale_gate, scale_up = pl.pallas_call(
+        gathered = pl.pallas_call(
             functools.partial(gather_kernel, count, pieces),
             out_shape=(block, block, scale, scale),
             in_specs=[held] * 4 + [vmem],
@@ -237,15 +258,25 @@
             scratch_shapes=[
                 pltpu.VMEM((2, rows, columns), jnp.float32),
                 pltpu.VMEM((2, rows, columns), jnp.float32),
-                pltpu.VMEM((count, 2, columns), jnp.float32),
-                dma(4 * pieces), dma(count - 1), dma(count - 1),
+                pltpu.VMEM((rows, LANES), jnp.float32),
+                pltpu.VMEM((2, count, 1, columns), jnp.float32),
+                dma(4 * pieces), dma(2 * count - 2), dma(2 * count - 2),
                 dma(line), dma(line), dma(line), dma(line), dma(wide), dma(wide), dma(pieces), dma(pieces),
             ],
             compiler_params=pltpu.CompilerParams(
-                collective_id=0, has_side_effects=True, vmem_limit_bytes=24 << 20
+                collective_id=0, has_side_effects=True,
+                vmem_limit_bytes=VMEM_BYTES - 2 * full[0] * full[1] * 2 - (1 << 19),
             ),
-        )(train_gate, slow_gate, train_up, slow_up, norm_gain[:, None])
-        return gate, up, scale_gate[0], scale_up[0]
+        )(train_gate, slow_gate, train_up, slow_up, norm_gain[None, :])
+        parts = 8
+        return pl.pallas_call(
+            functools.partial(store_kernel, parts),
+            out_shape=(jax.ShapeDtypeStruct(full, jnp.bfloat16),) * 2 + (jax.ShapeDtypeStruct((columns,), jnp.float32),) * 2,
+            in_specs=[vmem] * 4,
+            out_specs=(held, held, vmem, vmem),
+            scratch_shapes=[dma(2 * parts)],
+            compiler_params=pltpu.CompilerParams(vmem_limit_bytes=1 << 20),
+        )(*gathered)
 
     in_specs = (P("zero", "tp"), P("zero", "tp"), P("zero", "tp"), P("zero", "tp"), P("zero"))
     out_specs = (P(None, "tp"), P(None, "tp"), P("tp"), P("tp"))

time: 187 us -> 179 us (0.957)
  local copies, waits for them, and re-layouts: 15.2 us -> 0 us
  Pallas kernels: 171 us -> 178 us
    unnamed x12 -> x0, local copies, waits for them, and re-layouts: 14.4 us -> none
    pallas_call x0 -> x1, Pallas kernels: none -> 6.57 us  [body(): pl.pallas_call(functools.partial(store_kernel, parts), out_shape=(jax.Sha...]
where the time goes in v2:
time: 179 us
  Pallas kernels  178 us (99%)
    pallas_call x1, Pallas kernels, body(): pl.pallas_call(functools.partial(gather_kernel, count, pieces), out_shape...  172 us
    pallas_call x1, Pallas kernels, body(): pl.pallas_call(functools.partial(store_kernel, parts), out_shape=(jax.Sha...  6.57 us

profile of v2, /device:TPU:0, one launch (start us, length us, event | category | flops | bytes accessed | tf_op | source)
XLA Modules:
  0.0 178.7 jit_solution(1553996168305293529)
XLA Ops:
  0.6 171.5 %shard_map.84 = (bf16[2048,2048]{1,0:T(8,128)(2,1)S(1)}, bf16[2048,2048]{1,0:T(8,128)(2,1)S(1)}, f32[1,2048]{1,0:T(1,128)S(1)}, f32[1,2048]{1,0:T(1,128)S(1)}) custom-call(f32[256,2048]{1,0:T(8,128)} %train_gate.1, f32[256,2048]{1,0:T(8,128)} %slow_gate.1, f32[256,2048]{1,0:T(8,128)} %train_up.1, f32[256,2048]{1,0:T(8,128)} %slow_up.1, f32[1,256]{1,0:T(1,128)} %bitcast.1), custom_call_target="tpu_custom_call" | custom-call | tf_op jit(solution)/shard_map/pallas_call | solution.py:253
  172.2 6.6 %shard_map.85 = (bf16[2048,2048]{1,0:T(8,128)(2,1)}, bf16[2048,2048]{1,0:T(8,128)(2,1)}, f32[2048]{0:T(1024)}, f32[2048]{0:T(1024)}) custom-call(bf16[2048,2048]{1,0:T(8,128)(2,1)S(1)} %get-tuple-element.8.gate, bf16[2048,2048]{1,0:T(8,128)(2,1)S(1)} %get-tuple-element.9.up, f32[1,2048]{1,0:T(1,128)S(1)} %get-tuple-element.10.scale_gate, ...), custom_call_target="tpu_custom_call" | custom-call | tf_op jit(solution)/shard_map/pallas_call | solution.py:272

commit v3 on v2

--- a/solution.py
+++ b/solution.py
@@ -31,6 +31,10 @@
     outs = (gate_ref, up_ref)
     scales = (scale_gate_ref, scale_up_ref)
 
+    barrier = pltpu.get_barrier_semaphore()
+    for step in range(1, count):
+        pl.semaphore_signal(barrier, 1, device_id={"zero": lax.rem(me + step, count)}, device_id_type=MESH)
+
     loads = []
     for which, (t, s) in enumerate(((train_gate, slow_gate), (train_up, slow_up))):
         for p in range(pieces):
@@ -44,10 +48,6 @@
         for load in pair:
             load.start()
 
-    barrier = pltpu.get_barrier_semaphore()
-    for step in range(1, count):
-        pl.semaphore_signal(barrier, 1, device_id={"zero": lax.rem(me + step, count)}, device_id_type=MESH)
-
     gains[...] = jnp.broadcast_to(gain_ref[...], (LANES, rows)).T
 
     def sum_copy(which, step, source, to):
@@ -94,6 +94,7 @@
     is_even = place % 2 == 0
     twin = place + 1 - 2 * (place % 2)
     to_twin = twin * SIDE + side
+    half_round = jnp.maximum(jnp.where(is_even, place, length - 1 - place), 1)
     order = [(which, p) for which in range(2) for p in range(pieces)]
 
     def left_copy(distance, which, p):
@@ -190,10 +191,14 @@
             def _():
                 side_copy(-k, which, p).start()
 
-    for which, p in order:
-        side_arrival(0, which, p).wait_recv()
-        if which == 1:
-            half_copy(p).start()
+        @pl.when(half_round == k)
+        def _():
+            for p in range(pieces):
+                side_arrival(0, 1, p).wait_recv()
+                half_copy(p).start()
+
+    for p in range(pieces):
+        side_arrival(0, 0, p).wait_recv()
 
     for k in range(1, length):
         for which, p in order:
@@ -229,10 +234,10 @@
         for k in range(parts):
             at = pl.ds(k * rows, rows)
             copies.append(pltpu.make_async_copy(held.at[at], out.at[at], sem.at[which * parts + k]))
+    copies.append(pltpu.make_async_copy(scale_gate.at[0], scale_gate_out, sem.at[2 * parts]))
+    copies.append(pltpu.make_async_copy(scale_up.at[0], scale_up_out, sem.at[2 * parts + 1]))
     for copy in copies:
         copy.start()
-    scale_gate_out[...] = scale_gate[0, :]
-    scale_up_out[...] = scale_up[0, :]
     for copy in copies:
         copy.wait()
 
@@ -268,13 +273,13 @@
                 vmem_limit_bytes=VMEM_BYTES - 2 * full[0] * full[1] * 2 - (1 << 19),
             ),
         )(train_gate, slow_gate, train_up, slow_up, norm_gain[None, :])
-        parts = 8
+        parts = 4
         return pl.pallas_call(
             functools.partial(store_kernel, parts),
             out_shape=(jax.ShapeDtypeStruct(full, jnp.bfloat16),) * 2 + (jax.ShapeDtypeStruct((columns,), jnp.float32),) * 2,
             in_specs=[vmem] * 4,
-            out_specs=(held, held, vmem, vmem),
-            scratch_shapes=[dma(2 * parts)],
+            out_specs=(held,) * 4,
+            scratch_shapes=[dma(2 * parts + 2)],
             compiler_params=pltpu.CompilerParams(vmem_limit_bytes=1 << 20),
         )(*gathered)
 

time: 179 us -> 178 us (level)
  no operation moved by 1% of the time
where the time goes in v3:
time: 178 us
  Pallas kernels  177 us (99%)
    pallas_call x1, Pallas kernels, body(): pl.pallas_call(functools.partial(gather_kernel, count, pieces), out_shape...  172 us
    pallas_call x1, Pallas kernels, body(): pl.pallas_call(functools.partial(store_kernel, parts), out_shape=(jax.Sha...  5.95 us

profile of v3, /device:TPU:0, one launch (start us, length us, event | category | flops | bytes accessed | tf_op | source)
XLA Modules:
  0.0 178.1 jit_solution(5328310759787915185)
XLA Ops:
  0.6 171.5 %shard_map.84 = (bf16[2048,2048]{1,0:T(8,128)(2,1)S(1)}, bf16[2048,2048]{1,0:T(8,128)(2,1)S(1)}, f32[1,2048]{1,0:T(1,128)S(1)}, f32[1,2048]{1,0:T(1,128)S(1)}) custom-call(f32[256,2048]{1,0:T(8,128)} %train_gate.1, f32[256,2048]{1,0:T(8,128)} %slow_gate.1, f32[256,2048]{1,0:T(8,128)} %train_up.1, f32[256,2048]{1,0:T(8,128)} %slow_up.1, f32[1,256]{1,0:T(1,128)} %bitcast.1), custom_call_target="tpu_custom_call" | custom-call | tf_op jit(solution)/shard_map/pallas_call | solution.py:258
  172.2 5.9 %shard_map.85 = (bf16[2048,2048]{1,0:T(8,128)(2,1)}, bf16[2048,2048]{1,0:T(8,128)(2,1)}, f32[2048]{0:T(1024)}, f32[2048]{0:T(1024)}) custom-call(bf16[2048,2048]{1,0:T(8,128)(2,1)S(1)} %get-tuple-element.8.gate, bf16[2048,2048]{1,0:T(8,128)(2,1)S(1)} %get-tuple-element.9.up, f32[1,2048]{1,0:T(1,128)S(1)} %get-tuple-element.10.scale_gate, ...), custom_call_target="tpu_custom_call" | custom-call | tf_op jit(solution)/shard_map/pallas_call | solution.py:277

commit v4 on v3

--- a/solution.py
+++ b/solution.py
@@ -247,7 +247,7 @@
 
     def body(train_gate, slow_gate, train_up, slow_up, norm_gain):
         rows, columns = train_gate.shape
-        pieces = max(1, min(4, rows // 64))
+        pieces = max(1, min(2, rows // 64))
         length = count // SIDE
         full = (rows * count, columns)
         block = pltpu.VMEM(full, jnp.bfloat16)

time: 178 us -> 177 us (level)
  no operation moved by 1% of the time
where the time goes in v4:
time: 177 us
  Pallas kernels  177 us (100%)
    pallas_call x1, Pallas kernels, body(): pl.pallas_call(functools.partial(gather_kernel, count, pieces), out_shape...  171 us
    pallas_call x1, Pallas kernels, body(): pl.pallas_call(functools.partial(store_kernel, parts), out_shape=(jax.Sha...  5.95 us

profile of v4, /device:TPU:0, one launch (start us, length us, event | category | flops | bytes accessed | tf_op | source)
XLA Modules:
  0.0 177.2 jit_solution(4596102842945408140)
XLA Ops:
  0.6 170.6 %shard_map.84 = (bf16[2048,2048]{1,0:T(8,128)(2,1)S(1)}, bf16[2048,2048]{1,0:T(8,128)(2,1)S(1)}, f32[1,2048]{1,0:T(1,128)S(1)}, f32[1,2048]{1,0:T(1,128)S(1)}) custom-call(f32[256,2048]{1,0:T(8,128)} %train_gate.1, f32[256,2048]{1,0:T(8,128)} %slow_gate.1, f32[256,2048]{1,0:T(8,128)} %train_up.1, f32[256,2048]{1,0:T(8,128)} %slow_up.1, f32[1,256]{1,0:T(1,128)} %bitcast.1), custom_call_target="tpu_custom_call" | custom-call | tf_op jit(solution)/shard_map/pallas_call | solution.py:258
  171.2 5.9 %shard_map.85 = (bf16[2048,2048]{1,0:T(8,128)(2,1)}, bf16[2048,2048]{1,0:T(8,128)(2,1)}, f32[2048]{0:T(1024)}, f32[2048]{0:T(1024)}) custom-call(bf16[2048,2048]{1,0:T(8,128)(2,1)S(1)} %get-tuple-element.8.gate, bf16[2048,2048]{1,0:T(8,128)(2,1)S(1)} %get-tuple-element.9.up, f32[1,2048]{1,0:T(1,128)S(1)} %get-tuple-element.10.scale_gate, ...), custom_call_target="tpu_custom_call" | custom-call | tf_op jit(solution)/shard_map/pallas_call | solution.py:277

commit v5 on v4

--- a/solution.py
+++ b/solution.py
@@ -12,15 +12,17 @@
 SIDE = 2
 LANES = 128
 GROUP = 8
+HEAD = 16
+LEAD = 16
 VMEM_BYTES = 67_043_328
 
 
 def gather_kernel(
-    count, pieces,
+    count, pieces, head,
     train_gate, slow_gate, train_up, slow_up, gain_ref,
     gate_ref, up_ref, scale_gate_ref, scale_up_ref,
-    train, slow, gains, sums,
-    load_sem, sum_send, sum_recv,
+    train, slow, gains, sums, heads,
+    head_send, head_recv, load_sem, sum_send, sum_recv,
     left_send, left_recv, right_send, right_recv, side_send, side_recv, half_send, half_recv,
 ):
     length = count // SIDE
@@ -58,6 +60,10 @@
             device_id={"zero": to}, device_id_type=MESH,
         )
 
+    to_left = jnp.maximum(place - 1, 0) * SIDE + side
+    to_right = jnp.minimum(place + 1, length - 1) * SIDE + side
+    to_side = place * SIDE + (SIDE - 1 - side)
+    has_left, has_right = place > 0, place < length - 1
     for which in range(2):
         def add(i, total):
             at = pl.ds(pl.multiple_of(i * GROUP, GROUP), GROUP)
@@ -77,9 +83,30 @@
         for step in range(1, count):
             sum_copy(which, step, me, lax.rem(me + step, count)).start()
 
-    def part_of(owner_place, owner_side, which, p):
-        start = (owner_place * SIDE + owner_side) * rows + p * piece_rows
-        return outs[which].at[pl.ds(pl.multiple_of(start, piece_rows), piece_rows)]
+    def head_copy(slot, to):
+        return pltpu.make_async_remote_copy(
+            src_ref=slow.at[0, pl.ds(0, head)], dst_ref=heads.at[slot],
+            send_sem=head_send.at[slot], recv_sem=head_recv.at[slot],
+            device_id={"zero": to}, device_id_type=MESH,
+        )
+
+    @pl.when(has_left)
+    def _():
+        head_copy(0, to_left).start()
+
+    @pl.when(has_right)
+    def _():
+        head_copy(1, to_right).start()
+
+    head_copy(2, to_side).start()
+
+    def part_of(owner_place, owner_side, which, p, skip=0):
+        start = (owner_place * SIDE + owner_side) * rows + p * piece_rows + skip
+        step = GROUP * 2 if skip else piece_rows
+        return outs[which].at[pl.ds(pl.multiple_of(start, step), piece_rows - skip)]
+
+    def skipped(distance, which, p):
+        return head if (distance, which, p) == (0, 0, 0) else 0
 
     def copy_to(ref, send, recv, to):
         return pltpu.make_async_remote_copy(
@@ -87,10 +114,6 @@
             device_id={"zero": to}, device_id_type=MESH,
         )
 
-    to_left = jnp.maximum(place - 1, 0) * SIDE + side
-    to_right = jnp.minimum(place + 1, length - 1) * SIDE + side
-    to_side = place * SIDE + (SIDE - 1 - side)
-    has_left, has_right = place > 0, place < length - 1
     is_even = place % 2 == 0
     twin = place + 1 - 2 * (place % 2)
     to_twin = twin * SIDE + side
@@ -99,11 +122,11 @@
 
     def left_copy(distance, which, p):
         k = distance * 2 * pieces + which * pieces + p
-        return copy_to(part_of(place + distance, side, which, p), left_send.at[k], left_recv.at[k], to_left)
+        return copy_to(part_of(place + distance, side, which, p, skipped(distance, which, p)), left_send.at[k], left_recv.at[k], to_left)
 
     def right_copy(distance, which, p):
         k = distance * 2 * pieces + which * pieces + p
-        return copy_to(part_of(place - distance, side, which, p), right_send.at[k], right_recv.at[k], to_right)
+        return copy_to(part_of(place - distance, side, which, p, skipped(distance, which, p)), right_send.at[k], right_recv.at[k], to_right)
 
     def side_index(distance, which, p):
         d = distance if distance >= 0 else length - 1 - distance
@@ -111,11 +134,11 @@
 
     def side_copy(distance, which, p):
         k = side_index(distance, which, p)
-        return copy_to(part_of(place + distance, side, which, p), side_send.at[k], side_recv.at[k], to_side)
+        return copy_to(part_of(place + distance, side, which, p, skipped(distance, which, p)), side_send.at[k], side_recv.at[k], to_side)
 
     def side_arrival(distance, which, p):
         k = side_index(distance, which, p)
-        return copy_to(part_of(place + distance, SIDE - 1 - side, which, p), side_send.at[k], side_recv.at[k], to_side)
+        return copy_to(part_of(place + distance, SIDE - 1 - side, which, p, skipped(distance, which, p)), side_send.at[k], side_recv.at[k], to_side)
 
     def half_copy(p):
         return copy_to(part_of(place, SIDE - 1 - side, 1, p), half_send.at[p], half_recv.at[p], to_twin)
@@ -155,20 +178,41 @@
         scale = jnp.sqrt(total)
         scales[which][...] = scale
         inverse = 1.0 / scale
+        def store(p, first, size):
+            start = pl.multiple_of(me * rows + p * piece_rows + first, GROUP * 2)
+            block = slow[which, pl.ds(p * piece_rows + first, size), :]
+            outs[which][pl.ds(start, size), :] = (block * inverse).astype(jnp.bfloat16)
+
         for p in range(pieces + 1):
             if p < pieces:
-                at = pl.ds(p * piece_rows, piece_rows)
-                start = pl.multiple_of(me * rows + p * piece_rows, piece_rows)
-                outs[which][pl.ds(start, piece_rows), :] = (slow[which, at, :] * inverse).astype(jnp.bfloat16)
+                store(p, 0, LEAD)
             if p > 0:
                 send_own(which, p - 1)
+            if p < pieces:
+                store(p, LEAD, piece_rows - LEAD)
+
+        if which == 0:
+            def use_head(slot, owner, sender):
+                head_copy(slot, sender).wait_recv()
+                start = pl.multiple_of(owner * rows, GROUP * 2)
+                outs[0][pl.ds(start, head), :] = (heads[slot] * inverse).astype(jnp.bfloat16)
+
+            @pl.when(has_right)
+            def _():
+                use_head(0, to_right, to_right)
+
+            @pl.when(has_left)
+            def _():
+                use_head(1, to_left, to_left)
+
+            use_head(2, to_side, to_side)
 
     for k in range(1, length):
         for which, p in order:
             @pl.when(in_line(k))
             def _():
                 q = (k - 1) * 2 * pieces + which * pieces + p
-                copy_to(part_of(place + k, side, which, p), left_send.at[q], left_recv.at[q], to_right).wait_recv()
+                copy_to(part_of(place + k, side, which, p, skipped(k - 1, which, p)), left_send.at[q], left_recv.at[q], to_right).wait_recv()
 
                 @pl.when(has_left)
                 def _():
@@ -181,7 +225,7 @@
             @pl.when(in_line(-k))
             def _():
                 q = (k - 1) * 2 * pieces + which * pieces + p
-                copy_to(part_of(place - k, side, which, p), right_send.at[q], right_recv.at[q], to_left).wait_recv()
+                copy_to(part_of(place - k, side, which, p, skipped(k - 1, which, p)), right_send.at[q], right_recv.at[q], to_left).wait_recv()
 
                 @pl.when(has_right)
                 def _():
@@ -215,6 +259,16 @@
     for which in range(2):
         for step in range(1, count):
             sum_copy(which, step, me, lax.rem(me + step, count)).wait_send()
+
+    @pl.when(has_left)
+    def _():
+        head_copy(0, to_left).wait_send()
+
+    @pl.when(has_right)
+    def _():
+        head_copy(1, to_right).wait_send()
+
+    head_copy(2, to_side).wait_send()
     for which, p in order:
         side_copy(0, which, p).wait_send()
         for k in range(length):
@@ -248,6 +302,7 @@
     def body(train_gate, slow_gate, train_up, slow_up, norm_gain):
         rows, columns = train_gate.shape
         pieces = max(1, min(2, rows // 64))
+        head = HEAD
         length = count // SIDE
         full = (rows * count, columns)
         block = pltpu.VMEM(full, jnp.bfloat16)
@@ -256,7 +311,7 @@
         dma = lambda n: pltpu.SemaphoreType.DMA((n,))
         line, wide = length * 2 * pieces, (2 * length - 1) * 2 * pieces
         gathered = pl.pallas_call(
-            functools.partial(gather_kernel, count, pieces),
+            functools.partial(gather_kernel, count, pieces, head),
             out_shape=(block, block, scale, scale),
             in_specs=[held] * 4 + [vmem],
             out_specs=(vmem,) * 4,
@@ -265,7 +320,8 @@
                 pltpu.VMEM((2, rows, columns), jnp.float32),
                 pltpu.VMEM((rows, LANES), jnp.float32),
                 pltpu.VMEM((2, count, 1, columns), jnp.float32),
-                dma(4 * pieces), dma(2 * count - 2), dma(2 * count - 2),
+                pltpu.VMEM((3, head, columns), jnp.float32),
+                dma(3), dma(3), dma(4 * pieces), dma(2 * count - 2), dma(2 * count - 2),
                 dma(line), dma(line), dma(line), dma(line), dma(wide), dma(wide), dma(pieces), dma(pieces),
             ],
             compiler_params=pltpu.CompilerParams(

time: 177 us -> 177 us (level)
  no operation moved by 1% of the time
where the time goes in v5:
time: 177 us
  Pallas kernels  176 us (99%)
    pallas_call x1, Pallas kernels, body(): pl.pallas_call(functools.partial(gather_kernel, count, pieces, head), out...  170 us
    pallas_call x1, Pallas kernels, body(): pl.pallas_call(functools.partial(store_kernel, parts), out_shape=(jax.Sha...  5.95 us

profile of v5, /device:TPU:0, one launch (start us, length us, event | category | flops | bytes accessed | tf_op | source)
XLA Modules:
  0.0 177.0 jit_solution(1085924513938437617)
XLA Ops:
  0.6 170.4 %shard_map.84 = (bf16[2048,2048]{1,0:T(8,128)(2,1)S(1)}, bf16[2048,2048]{1,0:T(8,128)(2,1)S(1)}, f32[1,2048]{1,0:T(1,128)S(1)}, f32[1,2048]{1,0:T(1,128)S(1)}) custom-call(f32[256,2048]{1,0:T(8,128)} %train_gate.1, f32[256,2048]{1,0:T(8,128)} %slow_gate.1, f32[256,2048]{1,0:T(8,128)} %train_up.1, f32[256,2048]{1,0:T(8,128)} %slow_up.1, f32[1,256]{1,0:T(1,128)} %bitcast.1), custom_call_target="tpu_custom_call" | custom-call | tf_op jit(solution)/shard_map/pallas_call | solution.py:313
  171.0 5.9 %shard_map.85 = (bf16[2048,2048]{1,0:T(8,128)(2,1)}, bf16[2048,2048]{1,0:T(8,128)(2,1)}, f32[2048]{0:T(1024)}, f32[2048]{0:T(1024)}) custom-call(bf16[2048,2048]{1,0:T(8,128)(2,1)S(1)} %get-tuple-element.8.gate, bf16[2048,2048]{1,0:T(8,128)(2,1)S(1)} %get-tuple-element.9.up, f32[1,2048]{1,0:T(1,128)S(1)} %get-tuple-element.10.scale_gate, ...), custom_call_target="tpu_custom_call" | custom-call | tf_op jit(solution)/shard_map/pallas_call | solution.py:333
